TPU v7x, 32 devices: a whole 2x2x4 slice. The times are simulated.
32 devices in a mesh: member: 4 (over y, core), lat: 8 (over z, x).
Axes of the slice: x: 2, y: 2, z: 4, core: 2. Of those that a mesh axis runs over, the one named last changes fastest.
Arguments:
- ensemble: float32 [640, 32, 256], P('member', 'lat'), may hold values from -6 to 6
- obs_cell: int32 [32, 128], P(('member', 'lat')), may hold values from 0 to 255
- obs_value: float32 [32, 128], P(('member', 'lat')), may hold values from -8 to 8
- obs_var: float32 [32, 128], P(('member', 'lat')), may hold values from 0.5 to 8
- patch_rows: int32 [32, 2], P(('member', 'lat')), may hold values from 1 to 24, 32 in all within a row
Outputs:
- analysis: float32 [640, 32, 256], P('member', 'lat')
Inputs may be any that keep to these rules, and one draw needn't show every extreme that they name: `patch_rows`: each server's 2 patch lengths sum to 32.
All inputs are finite; a program needn't handle non-finite values. Where the computation divides by a largest or mean magnitude, that divisor is 1e-20 or more.
Results may differ from a plain program's by a relative error of at most 0.0003.
Values sent between devices are 32-bit elements; how exact they have to be, the bound alone decides.
A program may use at most 64 MiB of HBM per device.

v0:
```python
import jax
import jax.numpy as jnp
from jax import lax
from jax.sharding import PartitionSpec as P

STEPS = 4
lat_coeff = 0.4
lon_coeff = 0.05
advect_coeff = 0.1


def with_halo(value, sides, width, wrap):
    for axis, dim in sides:
        size, length = (lax.axis_size(axis), value.shape[dim])
        up = [(i, (i + 1) % size) for i in range(size if wrap else size - 1)]
        down = [(j, i) for i, j in up]
        last = lax.slice_in_dim(value, length - width, length, axis=dim)
        initial = lax.slice_in_dim(value, 0, width, axis=dim)
        before = lax.ppermute(last, axis, up)
        after = lax.ppermute(initial, axis, down)
        value = jnp.concatenate([before, value, after], axis=dim)
    return value


def advance(padded):
    centre = padded[:, 1:-1]
    northern = padded[:, :-2]
    southern = padded[:, 2:]
    eastern = jnp.roll(centre, -1, axis=2)
    western = jnp.roll(centre, 1, axis=2)
    return (
        centre
        + lat_coeff * (northern + southern - 2.0 * centre)
        + lon_coeff * (eastern + western - 2.0 * centre)
        - advect_coeff * centre * (eastern - western)
    )


def observe(states, cell_index, values):
    observed = jnp.take(states, cell_index, axis=1)
    obs_mean = jnp.mean(observed, axis=0)
    return (observed - obs_mean, values - obs_mean)


def localize(obs_rows, rel_cols, first_row, row_count, lat_scale, width_cols):
    lower = first_row.astype(jnp.float32)
    upper = lower + row_count.astype(jnp.float32) - 1.0
    lat_gap = jnp.maximum(jnp.maximum(lower - obs_rows, obs_rows - upper), 0.0) / lat_scale
    lon_gap = jnp.maximum(jnp.maximum(-rel_cols, rel_cols - (width_cols - 1.0)), 0.0) / width_cols
    return jnp.exp(-lat_gap * lat_gap - lon_gap * lon_gap)


def dot3(left, right):
    return jnp.matmul(left, right, precision=lax.Precision.HIGH, preferred_element_type=jnp.float32)


def analyse(states, spread, obs_meta, lengths, width_cols):
    members = states.shape[0]
    cell_total = states.shape[1]
    lat_total = cell_total // width_cols
    near = spread.shape[1]
    state_mean = jnp.mean(states, axis=0)
    anomaly = states - state_mean
    starts = jnp.cumsum(lengths) - lengths
    cell_rows = jnp.arange(cell_total, dtype=jnp.int32) // width_cols
    identity = jnp.eye(members, dtype=jnp.float32)
    products = dot3(spread.T, jnp.concatenate([spread, anomaly], axis=1))
    common, crossed = (products[:, :near], products[:, near:])
    innov = obs_meta[0]
    shrink = jnp.zeros((cell_total,), jnp.float32)
    shift = state_mean
    weights_all = jnp.zeros((near, cell_total), jnp.float32)
    for patch in range(lengths.shape[0]):
        weights = (
            localize(
                obs_meta[2],
                obs_meta[3],
                starts[patch],
                lengths[patch],
                lat_total / 4.0,
                float(width_cols),
            )
            / obs_meta[1]
        )
        scale = jnp.sqrt(weights)
        gram_matrix = (members - 1.0) * identity + jnp.dot(
            spread * weights, spread.T, preferred_element_type=jnp.float32
        )
        bound = jnp.max(jnp.sum(jnp.abs(gram_matrix), axis=1))
        alpha = (members - 1.0) / bound
        x = common * scale[:, None] * (scale / bound)[None, :]
        c0 = 2.25 + alpha * (-2.4375 + alpha * (1.6875 + alpha * (-0.5625 + alpha * 0.0625)))
        c1 = -2.4375 + alpha * (3.375 + alpha * (-1.6875 + alpha * 0.25))
        c2 = 1.6875 + alpha * (-1.6875 + alpha * 0.375)
        c3 = -0.5625 + alpha * 0.25
        c4 = 0.0625
        x2 = dot3(x, x)
        x34 = dot3(x2, jnp.concatenate([x, x2], axis=1))
        x3, x4 = (x34[:, :near], x34[:, near:])
        low = c2 * x + c3 * x2 + c4 * x3
        high = c1 * x + c2 * x2 + c3 * x3 + c4 * x4
        block = jnp.concatenate([crossed * scale[:, None], (scale * innov)[:, None]], axis=1)
        both = dot3(jnp.concatenate([low, high], axis=0), block)
        b1 = c1 * block + both[:near]
        b2 = c0 * block + both[near:]
        b3 = c0 * b2 + dot3(high, b2)
        mixed = alpha * c0 * b1 + b3
        got = 1.5 * b1 - 0.5 * (
            alpha * c0 * c0 * b1
            + c0 * mixed
            + dot3(high, mixed)
            + alpha * (c1 * b3 + dot3(low, b3))
        )
        base = c0 * (1.5 - 0.5 * alpha * c0 * c0)
        driven = base * block[:, -1] + jnp.sum(x * got[:, -1][None, :], axis=1)
        again = jnp.sum(x * driven[None, :], axis=1)
        mean_part = (
            jnp.sum(block[:, :-1] * (base * driven)[:, None] + got[:, :-1] * again[:, None], axis=0)
            / bound
        )
        cell_mask = (cell_rows >= starts[patch]) & (cell_rows < starts[patch] + lengths[patch])
        root_scale = jnp.sqrt((members - 1.0) / bound)
        shift = shift + jnp.where(cell_mask, mean_part, 0.0)
        shrink = jnp.where(cell_mask, root_scale * base, shrink)
        weights_all = jnp.where(
            cell_mask[None, :], got[:, :-1] * (scale * (root_scale / bound))[:, None], weights_all
        )
    return shift + shrink * anomaly + dot3(spread, weights_all)


def per_device(ensemble, obs_cell, obs_value, obs_var, patch_rows):
    fields = ensemble
    members_dev = fields.shape[0]
    lat_rows = fields.shape[1]
    lon_cells = fields.shape[2]
    lat_count = lax.axis_size("lat")
    member_count = lax.axis_size("member")
    servers = lat_count * member_count
    width_cols = lon_cells // servers
    padded = with_halo(fields, (("lat", 1),), STEPS, False)
    global_rows = (
        lax.axis_index("lat") * lat_rows + jnp.arange(lat_rows + 2 * STEPS, dtype=jnp.int32) - STEPS
    )
    inside = ((global_rows >= 0) & (global_rows < lat_rows * lat_count)).astype(jnp.float32)
    for step_index in range(STEPS):
        padded = advance(padded)
        keeper = inside[step_index + 1 : inside.shape[0] - step_index - 1]
        padded = padded * keeper[None, :, None]
    fields = padded
    blocks = fields.reshape(1, members_dev, lat_rows, lon_cells)
    received = lax.all_to_all(blocks, ("member", "lat"), split_axis=3, concat_axis=0, tiled=True)
    strip = received.reshape(member_count, lat_count, members_dev, lat_rows, width_cols)
    strip = strip.transpose(0, 2, 1, 3, 4).reshape(
        member_count * members_dev, lat_count * lat_rows, width_cols
    )
    members = strip.shape[0]
    lat_total = strip.shape[1]
    states = strip.reshape(members, lat_total * width_cols)
    cell_index = obs_cell[0]
    obs_count = cell_index.shape[0]
    spread, innov = observe(states, cell_index, obs_value[0])
    obs_meta = jnp.stack(
        [
            innov,
            obs_var[0],
            (cell_index // width_cols).astype(jnp.float32),
            (cell_index % width_cols).astype(jnp.float32),
        ]
    )
    near_spread, near_meta = (
        with_halo(spread, ((("member", "lat"), 1),), obs_count, True),
        with_halo(obs_meta, ((("member", "lat"), 1),), obs_count, True),
    )
    shifts = jnp.repeat(jnp.array([-1.0, 0.0, 1.0], jnp.float32), obs_count) * width_cols
    near_meta = jnp.concatenate([near_meta[:3], (near_meta[3] + shifts)[None, :]], axis=0)
    analysed = analyse(states, near_spread, near_meta, patch_rows[0], width_cols)
    analysed = analysed.reshape(members, lat_total, width_cols)
    outgoing = analysed.reshape(member_count, members_dev, lat_count, lat_rows, width_cols)
    outgoing = outgoing.transpose(0, 2, 1, 3, 4).reshape(servers, members_dev, lat_rows, width_cols)
    returned = lax.all_to_all(outgoing, ("member", "lat"), split_axis=0, concat_axis=3, tiled=True)
    return returned.reshape(members_dev, lat_rows, lon_cells)


def solution(mesh):
    in_specs = (
        P("member", "lat", None),
        P(("member", "lat"), None),
        P(("member", "lat"), None),
        P(("member", "lat"), None),
        P(("member", "lat"), None),
    )
    out_specs = P("member", "lat", None)
    return jax.shard_map(
        per_device, mesh=mesh, in_specs=in_specs, out_specs=out_specs, check_vma=False
    )
```

profile of v0, /device:TPU:0, one launch (start us, length us, event | category | flops | bytes accessed | tf_op | source)
XLA Modules:
  0.0 164.4 jit_solution(16774635268156717155)
XLA Ops:
  0.0 1.3 copy.83
  1.3 4.9 %collective-permute-start = (f32[160,4,256]{2,0,1:T(8,128)S(1)}, f32[160,4,256]{2,0,1:T(8,128)S(1)}, u32[]{:S(2)}, u32[]{:S(2)}) collective-permute-start(f32[160,4,256]{2,0,1:T(8,128)S(1)} %copy.83), channel_id=1, source_target_pairs={{0,1},{1,2},{2,3},{3,4},{4,5},{5,6},{6,7},{8,9},{9,10},{10,11},{11... | collective-permute-start | bytes 1966088 | tf_op jit(solution)/shard_map/ppermute | solution.py:19
  6.2 1.3 collective-permute-start.1
  7.8 0.8 reduce-window.9
  8.6 25.5 %collective-permute-done = f32[160,4,256]{2,0,1:T(8,128)S(1)} collective-permute-done((f32[160,4,256]{2,0,1:T(8,128)S(1)}, f32[160,4,256]{2,0,1:T(8,128)S(1)}, u32[]{:S(2)}, u32[]{:S(2)}) %collective-permute-start) | collective-permute-done | bytes 655392 | tf_op jit(solution)/shard_map/ppermute | solution.py:19
  35.3 1.1 fusion.9
  37.0 0.9 fusion.25
  38.4 0.7 fusion.55
  40.1 1.3 copy.86
  41.4 6.6 %all-to-all-start = ((f32[1,160,4,256]{1,2,0,3:T(4,128)}), f32[1,160,4,256]{1,2,0,3:T(4,128)S(1)}, u32[]{:S(2)}, u32[]{:S(2)}) async-start(f32[1,160,4,256]{1,2,0,3:T(4,128)} %copy.86), calls=%async_computation | async-start | bytes 2097152 | tf_op jit(solution)/shard_map/all_to_all | solution.py:151
  48.0 0.6 fusion.135
  49.2 0.6 fusion.134
  54.3 21.2 %all-to-all-done = f32[1,160,4,256]{1,2,0,3:T(4,128)S(1)} async-done(((f32[1,160,4,256]{1,2,0,3:T(4,128)}), f32[1,160,4,256]{1,2,0,3:T(4,128)S(1)}, u32[]{:S(2)}, u32[]{:S(2)}) %all-to-all-start) | async-done | bytes 655392 | tf_op jit(solution)/shard_map/all_to_all | solution.py:151
  75.7 0.7 copy.89
  76.4 0.6 reshape_reshape.6
  77.0 0.8 gather_fusion
  78.2 0.8 collective-permute-start.4
  79.0 4.6 %collective-permute-start.5 = (f32[4,128]{1,0:T(4,128)S(1)}, f32[4,128]{1,0:T(4,128)S(1)}, u32[]{:S(2)}, u32[]{:S(2)}) collective-permute-start(f32[4,128]{1,0:T(4,128)S(1)} %pad_maximum_fusion.22), channel_id=1, source_target_pairs={{1,0},{2,1},{3,2},{4,3},{5,4},{6,5},{7,6},{8,7},{9,8},{10,9},{11,1... | collective-permute-start | bytes 6152 | tf_op jit(solution)/shard_map/ppermute | solution.py:20
  83.7 5.3 %collective-permute-start.3 = (f32[640,128]{1,0:T(8,128)S(1)}, f32[640,128]{1,0:T(8,128)}, u32[]{:S(2)}, u32[]{:S(2)}) collective-permute-start(f32[640,128]{1,0:T(8,128)S(1)} %subtract_bitcast_fusion), channel_id=1, source_target_pairs={{1,0},{2,1},{3,2},{4,3},{5,4},{6,5},{7,6},{8,7},{9,8},{10,9},{11,1... | collective-permute-start | bytes 983048 | tf_op jit(solution)/shard_map/ppermute | solution.py:20
  90.4 6.6 %collective-permute-done.2 = f32[640,128]{1,0:T(8,128)S(1)} collective-permute-done((f32[640,128]{1,0:T(8,128)S(1)}, f32[640,128]{1,0:T(8,128)S(1)}, u32[]{:S(2)}, u32[]{:S(2)}) %collective-permute-start.2) | collective-permute-done | bytes 327712 | tf_op jit(solution)/shard_map/ppermute | solution.py:19
  97.0 2.5 %collective-permute-done.3 = f32[640,128]{1,0:T(8,128)} collective-permute-done((f32[640,128]{1,0:T(8,128)S(1)}, f32[640,128]{1,0:T(8,128)}, u32[]{:S(2)}, u32[]{:S(2)}) %collective-permute-start.3) | collective-permute-done | bytes 327712 | tf_op jit(solution)/shard_map/ppermute | solution.py:20
  99.5 1.8 %fusion.3 = f32[640]{0:T(1024)S(1)} fusion(f32[640,128]{1,0:T(8,128)} %collective-permute-done.3, f32[640,128]{1,0:T(8,128)S(1)} %subtract_bitcast_fusion, f32[640,128]{1,0:T(8,128)S(1)} %collective-permute-done.2, f32[384]{0:T(512)S(1)} %get-tuple-element.25), kind=kOutput, calls=%fused_computation.6 | convolution fusion | flops 317848960 | bytes 987136 | tf_op jit(solution)/shard_map/dot_general | solution.py:86
  101.3 0.7 reduce_max.19
  102.7 1.8 %fusion.1 = f32[640]{0:T(1024)S(1)} fusion(f32[640,128]{1,0:T(8,128)} %collective-permute-done.3, f32[640,128]{1,0:T(8,128)S(1)} %subtract_bitcast_fusion, f32[640,128]{1,0:T(8,128)S(1)} %collective-permute-done.2, f32[384]{0:T(512)S(1)} %get-tuple-element.53), kind=kOutput, calls=%fused_computation.4 | convolution fusion | flops 317848960 | bytes 987136 | tf_op jit(solution)/shard_map/dot_general | solution.py:86
  104.5 0.6 reduce_max.18
  107.2 0.7 divide_reduce_fusion
  107.9 0.6 divide_reduce_fusion.1
  108.6 0.7 broadcast_multiply_fusion.1
  109.3 2.6 %fusion.10 = f32[384,640]{1,0:T(8,128)S(1)} fusion(f32[640,256]{1,0:T(8,128)S(1)} %broadcast_subtract_fusion, f32[640,128]{1,0:T(8,128)} %collective-permute-done.3, f32[640,128]{1,0:T(8,128)S(1)} %subtract_bitcast_fusion, f32[640,128]{1,0:T(8,128)S(1)} %collective-permute-done.2), kind=kOutput, calls=%fused_computation.16 | convolution fusion | flops 945438720 | bytes 2621440 | tf_op jit(solution)/shard_map/dot_general | solution.py:54
  112.3 0.7 fusion.136
  113.0 0.8 copy-done
  113.9 2.1 %fusion.34 = f32[384,768]{1,0:T(8,128)} fusion(f32[384,384]{1,0:T(8,128)S(1)} %fusion.136, f32[384,384]{1,0:T(8,128)S(1)} %get-tuple-element.47), kind=kOutput, calls=%fused_computation.51 | convolution fusion | flops 679772160 | bytes 2359296 | tf_op jit(solution)/shard_map/dot_general | solution.py:54
  116.0 0.7 fusion.137
  116.7 1.1 fusion.42
  118.4 1.3 fusion.46
  119.6 0.8 convolution_add_fusion.3
  120.4 0.7 fusion.33
  121.2 1.0 fusion.32
  122.1 0.8 copy-done.3
  123.2 1.5 fusion.38
  124.7 0.8 convolution_add_fusion.6
  125.5 0.7 fusion.29
  126.3 0.9 fusion.28
  128.4 2.4 %fusion.104 = (f32[256]{0:T(256)S(1)}, pred[256]{0:T(512)(128)(4,1)S(1)}, pred[256]{0:T(512)(128)(4,1)S(1)}) fusion(f32[256]{0:T(256)S(1)} %add_reduce_fusion, f32[256]{0:T(256)S(1)} %copy-done.17, f32[256]{0:T(256)S(1)} %add_reduce_fusion.1, f32[]{:T(128)} %reduce_max.19, f32[]{:T(128)} %reduce_max.18, s32[]{:T(128)S(6)} %add.404, s32[]{:T(128)} %bitcast.8, ...), kind=kLoop, calls=%fused_computation.203 | loop fusion | flops 5120 | bytes 4632 | tf_op jit(solution)/shard_map/add | solution.py:123
  130.9 1.8 %convolution_add_fusion = f32[640,256]{1,0:T(8,128)S(1)} fusion(f32[640,256]{1,0:T(8,128)S(1)} %copy-done.7, f32[640,128]{1,0:T(8,128)} %collective-permute-done.3, f32[640,128]{1,0:T(8,128)S(1)} %copy-done.9, f32[640,128]{1,0:T(8,128)S(1)} %copy-done.11, f32[384,257]{1,0:T(8,128)S(1)} %copy-done.4, f32[384,257]{1,0:T(8,128)S(1)} %fusion.28, ...), kind=kOutput, calls=%fused_computation.36 | convolution fusion | flops 378863616 | bytes 3087360 | tf_op jit(solution)/shard_map/dot_general | solution.py:54
  132.9 0.7 reshape_reshape.7
  133.9 29.2 %all_to_all.30 = f32[32,160,4,8]{1,3,2,0:T(8,128)S(1)} all-to-all(f32[32,160,4,8]{1,3,2,0:T(8,128)S(1)} %bitcast.110), channel_id=1, replica_groups=mesh['member'=4,'lat'=8] {'member','lat'}, dimensions={0} | all-to-all | bytes 1310720 | tf_op jit(solution)/shard_map/all_to_all | solution.py:180
  163.2 1.1 copy.107
  (112 shorter events, 8.3 us)
Async XLA Ops:
  0.0 34.2 %copy-start.5 = (f32[160,4,256]{2,1,0:T(4,128)S(1)}, f32[160,4,256]{2,1,0:T(4,128)}, u32[]{:S(2)}) copy-start(f32[160,4,256]{2,1,0:T(4,128)} %param.6) | copy-start | bytes 1966084
  1.3 32.9 %collective-permute-start = (f32[160,4,256]{2,0,1:T(8,128)S(1)}, f32[160,4,256]{2,0,1:T(8,128)S(1)}, u32[]{:S(2)}, u32[]{:S(2)}) collective-permute-start(f32[160,4,256]{2,0,1:T(8,128)S(1)} %copy.83), channel_id=1, source_target_pairs={{0,1},{1,2},{2,3},{3,4},{4,5},{5,6},{6,7},{8,9},{9,10},{10,11},{11... | collective-permute-start | bytes 1966088 | tf_op jit(solution)/shard_map/ppermute | solution.py:19
  6.2 28.2 %collective-permute-start.1 = (f32[160,4,256]{2,0,1:T(8,128)S(1)}, f32[160,4,256]{2,0,1:T(8,128)S(1)}, u32[]{:S(2)}, u32[]{:S(2)}) collective-permute-start(f32[160,4,256]{2,0,1:T(8,128)S(1)} %copy.83), channel_id=1, source_target_pairs={{1,0},{2,1},{3,2},{4,3},{5,4},{6,5},{7,6},{9,8},{10,9},{11,10},{12... | collective-permute-start | bytes 1966088 | tf_op jit(solution)/shard_map/ppermute | solution.py:20
  40.0 8.0 %copy-start.21 = (s32[1,2]{1,0:T(1,128)S(1)}, s32[1,2]{1,0:T(1,128)}, u32[]{:S(2)}) copy-start(s32[1,2]{1,0:T(1,128)} %param.10) | copy-start | bytes 28
  40.0 14.1 %copy-start.23 = (s32[1,128]{1,0:T(1,128)S(1)}, s32[1,128]{1,0:T(1,128)}, u32[]{:S(2)}) copy-start(s32[1,128]{1,0:T(1,128)} %param.7) | copy-start | bytes 1540
  40.1 14.1 %copy-start.20 = (f32[3]{0:T(128)S(1)}, f32[3]{0:T(128)}, u32[]{:S(2)}) copy-start(f32[3]{0:T(128)} %constant.157) | copy-start | bytes 40
  41.4 34.1 %all-to-all-start = ((f32[1,160,4,256]{1,2,0,3:T(4,128)}), f32[1,160,4,256]{1,2,0,3:T(4,128)S(1)}, u32[]{:S(2)}, u32[]{:S(2)}) async-start(f32[1,160,4,256]{1,2,0,3:T(4,128)} %copy.86), calls=%async_computation | async-start | bytes 2097152 | tf_op jit(solution)/shard_map/all_to_all | solution.py:151
  77.0 1.1 copy-start.24
  77.0 1.1 copy-start.22
  78.2 11.6 %collective-permute-start.4 = (f32[4,128]{1,0:T(4,128)S(1)}, f32[4,128]{1,0:T(4,128)S(1)}, u32[]{:S(2)}, u32[]{:S(2)}) collective-permute-start(f32[4,128]{1,0:T(4,128)S(1)} %pad_maximum_fusion.22), channel_id=1, source_target_pairs={{0,1},{1,2},{2,3},{3,4},{4,5},{5,6},{6,7},{7,8},{8,9},{9,10},{10,1... | collective-permute-start | bytes 6152 | tf_op jit(solution)/shard_map/ppermute | solution.py:19
  79.0 10.7 %collective-permute-start.5 = (f32[4,128]{1,0:T(4,128)S(1)}, f32[4,128]{1,0:T(4,128)S(1)}, u32[]{:S(2)}, u32[]{:S(2)}) collective-permute-start(f32[4,128]{1,0:T(4,128)S(1)} %pad_maximum_fusion.22), channel_id=1, source_target_pairs={{1,0},{2,1},{3,2},{4,3},{5,4},{6,5},{7,6},{8,7},{9,8},{10,9},{11,1... | collective-permute-start | bytes 6152 | tf_op jit(solution)/shard_map/ppermute | solution.py:20
  83.6 25.7 %copy-start.8 = (f32[640,128]{1,0:T(8,128)}, f32[640,128]{1,0:T(8,128)S(1)}, u32[]{:S(2)}) copy-start(f32[640,128]{1,0:T(8,128)S(1)} %subtract_bitcast_fusion) | copy-start | bytes 983044
  83.6 13.4 %collective-permute-start.2 = (f32[640,128]{1,0:T(8,128)S(1)}, f32[640,128]{1,0:T(8,128)S(1)}, u32[]{:S(2)}, u32[]{:S(2)}) collective-permute-start(f32[640,128]{1,0:T(8,128)S(1)} %subtract_bitcast_fusion), channel_id=1, source_target_pairs={{0,1},{1,2},{2,3},{3,4},{4,5},{5,6},{6,7},{7,8},{8,9},{9,10},{10,1... | collective-permute-start | bytes 983048 | tf_op jit(solution)/shard_map/ppermute | solution.py:19
  83.7 15.8 %collective-permute-start.3 = (f32[640,128]{1,0:T(8,128)S(1)}, f32[640,128]{1,0:T(8,128)}, u32[]{:S(2)}, u32[]{:S(2)}) collective-permute-start(f32[640,128]{1,0:T(8,128)S(1)} %subtract_bitcast_fusion), channel_id=1, source_target_pairs={{1,0},{2,1},{3,2},{4,3},{5,4},{6,5},{7,6},{8,7},{9,8},{10,9},{11,1... | collective-permute-start | bytes 983048 | tf_op jit(solution)/shard_map/ppermute | solution.py:20
  89.6 0.6 copy-start.16
  89.7 19.6 %copy-start.6 = (f32[640,256]{1,0:T(8,128)}, f32[640,256]{1,0:T(8,128)S(1)}, u32[]{:S(2)}) copy-start(f32[640,256]{1,0:T(8,128)S(1)} %broadcast_subtract_fusion) | copy-start | bytes 1966084
  89.8 18.1 %copy-start.12 = (f32[1,384]{1,0:T(1,128)}, f32[1,384]{1,0:T(1,128)S(1)}, u32[]{:S(2)}) copy-start(f32[1,384]{1,0:T(1,128)S(1)} %get-tuple-element.54) | copy-start | bytes 4612
  90.4 16.8 %copy-start.14 = (f32[1,384]{1,0:T(1,128)}, f32[1,384]{1,0:T(1,128)S(1)}, u32[]{:S(2)}) copy-start(f32[1,384]{1,0:T(1,128)S(1)} %get-tuple-element.26) | copy-start | bytes 4612
  97.0 12.3 %copy-start.10 = (f32[640,128]{1,0:T(8,128)}, f32[640,128]{1,0:T(8,128)S(1)}, u32[]{:S(2)}) copy-start(f32[640,128]{1,0:T(8,128)S(1)} %collective-permute-done.2) | copy-start | bytes 983044
  113.0 0.8 copy-start
  116.0 1.9 %copy-start.1 = (f32[384,384]{1,0:T(8,128)S(1)}, f32[384,384]{1,0:T(8,128)}, u32[]{:S(2)}) copy-start(f32[384,384]{1,0:T(8,128)} %copy-done) | copy-start | bytes 1769476
  116.0 1.9 %copy-start.2 = (f32[384,768]{1,0:T(8,128)S(1)}, f32[384,768]{1,0:T(8,128)}, u32[]{:S(2)}) copy-start(f32[384,768]{1,0:T(8,128)} %fusion.34) | copy-start | bytes 3538948
  122.1 0.8 copy-start.3
  126.2 1.3 copy-start.13
  126.2 1.3 copy-start.15
  127.2 1.1 copy-start.4
  127.3 1.1 copy-start.17
  127.4 3.5 %copy-start.7 = (f32[640,256]{1,0:T(8,128)S(1)}, f32[640,256]{1,0:T(8,128)}, u32[]{:S(2)}) copy-start(f32[640,256]{1,0:T(8,128)} %copy-done.6) | copy-start | bytes 1966084
  127.4 3.5 %copy-start.9 = (f32[640,128]{1,0:T(8,128)S(1)}, f32[640,128]{1,0:T(8,128)}, u32[]{:S(2)}) copy-start(f32[640,128]{1,0:T(8,128)} %copy-done.8) | copy-start | bytes 983044
  127.4 3.5 %copy-start.11 = (f32[640,128]{1,0:T(8,128)S(1)}, f32[640,128]{1,0:T(8,128)}, u32[]{:S(2)}) copy-start(f32[640,128]{1,0:T(8,128)} %copy-done.10) | copy-start | bytes 983044
  127.4 3.5 %copy-start.18 = (f32[384]{0:T(512)S(1)}, f32[384]{0:T(512)}, u32[]{:S(2)}) copy-start(f32[384]{0:T(512)} %get-tuple-element.12) | copy-start | bytes 4612
  127.4 3.5 %copy-start.19 = (f32[384]{0:T(512)S(1)}, f32[384]{0:T(512)}, u32[]{:S(2)}) copy-start(f32[384]{0:T(512)} %get-tuple-element.56) | copy-start | bytes 4612
where the time goes:
time: 165 us; the launch traced here: 164 us
  waiting for transfers between devices  55.9 us (34%)
  blocking collectives  29.2 us (18%)
  starting transfers between devices  23.6 us (14%)
  matrix products  20.3 us (12%)
  local copies, waits for them, and re-layouts  14.7 us (9%)
  other arithmetic  12.1 us (7%)
  between operations  8.58 us (5%)
    ppermute x3, waiting for transfers between devices, with_halo(): before = lax.ppermute(last, axis, up)  32.1 us
    all_to_all x1, blocking collectives, per_device(): lax.all_to_all(outgoing, ('member', 'lat'), split_axis=0, concat_axis=3,...  29.2 us
    all_to_all x1, waiting for transfers between devices, per_device(): lax.all_to_all(blocks, ('member', 'lat'), split_axis=3, concat_axis=0, ti...  21.2 us
    dot_general x14, matrix products, dot3(): jnp.matmul(left, right, precision=lax.Precision.HIGH, preferred_element_t...  16.7 us
    ppermute x3, starting transfers between devices, with_halo(): after = lax.ppermute(initial, axis, down)  11.2 us
    all_to_all x1, starting transfers between devices, per_device(): lax.all_to_all(blocks, ('member', 'lat'), split_axis=3, concat_axis=0, ti...  6.62 us
    ppermute x3, starting transfers between devices, with_halo(): before = lax.ppermute(last, axis, up)  5.8 us
    unnamed x54, local copies, waits for them, and re-layouts  3.6 us
  transfers between devices with their start and end apart: 7, of which 4 were waited for; matrix products, arithmetic and copies ran while one was open for 2% of the time, Pallas kernels for 0%

commit v1 on v0

--- a/solution.py
+++ b/solution.py
@@ -1,3 +1,4 @@
+import functools
 import jax
 import jax.numpy as jnp
 from jax import lax
@@ -7,6 +8,16 @@
 lat_coeff = 0.4
 lon_coeff = 0.05
 advect_coeff = 0.1
+
+
+def keep_up_the_shifts_all(my_tile, dim_k, join_dim):
+    w2 = lax.axis_size(("member", "lat"))
+    y1 = jnp.split(my_tile, w2, dim_k)
+    q_next = lax.all_to_all(jnp.stack(y1, axis=0), ("member", "lat"), 0, 0)
+    return jnp.concatenate(q_next, axis=join_dim)
+
+
+screen_supply = functools.partial(keep_up_the_shifts_all, dim_k=3, join_dim=0)
 
 
 def with_halo(value, sides, width, wrap):
@@ -148,7 +159,7 @@
         padded = padded * keeper[None, :, None]
     fields = padded
     blocks = fields.reshape(1, members_dev, lat_rows, lon_cells)
-    received = lax.all_to_all(blocks, ("member", "lat"), split_axis=3, concat_axis=0, tiled=True)
+    received = screen_supply(blocks)
     strip = received.reshape(member_count, lat_count, members_dev, lat_rows, width_cols)
     strip = strip.transpose(0, 2, 1, 3, 4).reshape(
         member_count * members_dev, lat_count * lat_rows, width_cols

time: 165 us -> 221 us (1.34)
  local copies, waits for them, and re-layouts: 14.7 us -> 73.7 us
  matrix products: 20.3 us -> 16.1 us
    another operation x0 -> x36, local copies, waits for them, and re-layouts: none -> 42.7 us  [the longest x35 42 us: keep_up_the_shifts_all(): q_next = lax.all_to_all(jnp.stack(y1, axis=0), ('member', 'lat'), 0, 0)]
    unnamed x54 -> x119, local copies, waits for them, and re-layouts: 3.6 us -> 22.3 us
where the time goes in v1:
time: 221 us; the launch traced here: 219 us
  local copies, waits for them, and re-layouts  73.7 us (33%)
  waiting for transfers between devices  54.8 us (25%)
  blocking collectives  29.2 us (13%)
  starting transfers between devices  23.8 us (11%)
  matrix products  16.1 us (7%)
  other arithmetic  13 us (6%)
  between operations  8.67 us (4%)
    another operation x35, local copies, waits for them, and re-layouts, keep_up_the_shifts_all(): q_next = lax.all_to_all(jnp.stack(y1, axis=0), ('member', 'lat'), 0, 0)  42 us
    ppermute x3, waiting for transfers between devices, with_halo(): before = lax.ppermute(last, axis, up)  31.5 us
    all_to_all x1, blocking collectives, per_device(): lax.all_to_all(outgoing, ('member', 'lat'), split_axis=0, concat_axis=3,...  29.2 us
    unnamed x119, local copies, waits for them, and re-layouts  22.3 us
    all_to_all x1, waiting for transfers between devices, keep_up_the_shifts_all(): q_next = lax.all_to_all(jnp.stack(y1, axis=0), ('member', 'lat'), 0, 0)  21 us
    dot_general x14, matrix products, dot3(): jnp.matmul(left, right, precision=lax.Precision.HIGH, preferred_element_t...  14.7 us
    ppermute x3, starting transfers between devices, with_halo(): after = lax.ppermute(initial, axis, down)  11.2 us
    all_to_all x1, starting transfers between devices, keep_up_the_shifts_all(): q_next = lax.all_to_all(jnp.stack(y1, axis=0), ('member', 'lat'), 0, 0)  6.8 us
  transfers between devices with their start and end apart: 7, of which 4 were waited for; matrix products, arithmetic and copies ran while one was open for 2% of the time, Pallas kernels for 0%

profile of v1, /device:TPU:0, one launch (start us, length us, event | category | flops | bytes accessed | tf_op | source)
XLA Modules:
  0.0 219.3 jit_solution(9949395641370279676)
XLA Ops:
  0.0 1.3 copy.139
  1.3 4.9 %collective-permute-start = (f32[160,4,256]{2,0,1:T(8,128)S(1)}, f32[160,4,256]{2,0,1:T(8,128)S(1)}, u32[]{:S(2)}, u32[]{:S(2)}) collective-permute-start(f32[160,4,256]{2,0,1:T(8,128)S(1)} %copy.139), channel_id=1, source_target_pairs={{0,1},{1,2},{2,3},{3,4},{4,5},{5,6},{6,7},{8,9},{9,10},{10,11},{11... | collective-permute-start | bytes 1966088 | tf_op jit(solution)/shard_map/ppermute | solution.py:30
  6.2 1.3 collective-permute-start.1
  8.6 25.5 %collective-permute-done = f32[160,4,256]{2,0,1:T(8,128)S(1)} collective-permute-done((f32[160,4,256]{2,0,1:T(8,128)S(1)}, f32[160,4,256]{2,0,1:T(8,128)S(1)}, u32[]{:S(2)}, u32[]{:S(2)}) %collective-permute-start) | collective-permute-done | bytes 655392 | tf_op jit(solution)/shard_map/ppermute | solution.py:30
  35.3 1.1 fusion.9
  37.0 0.9 fusion.25
  40.0 3.1 %slice_bitcast_fusion.19 = (f32[1,1,160,4,8]{4,2,3,1,0:T(8,128)}, f32[1,1,160,4,8]{4,2,3,1,0:T(8,128)}, f32[1,1,160,4,8]{4,2,3,1,0:T(8,128)}, f32[1,1,160,4,8]{4...) fusion(f32[1,160,4,256]{3,1,2,0:T(8,128)S(1)} %fusion.62), kind=kLoop, calls=%fused_computation.146 | loop fusion | bytes 532480 | tf_op jit(solution)/shard_map/stack | solution.py:16
  43.1 3.1 %slice_bitcast_fusion = (f32[1,1,160,4,8]{4,2,3,1,0:T(8,128)S(1)}, f32[1,1,160,4,8]{4,2,3,1,0:T(8,128)S(1)}, f32[1,1,160,4,8]{4,2,3,1,0:T(8,128)S(1)}, f32[1,1,1...) fusion(f32[1,160,4,256]{3,1,2,0:T(8,128)S(1)} %fusion.62), kind=kLoop, calls=%fused_computation.127 | loop fusion | bytes 778240 | tf_op jit(solution)/shard_map/stack | solution.py:16
  46.2 1.1 copy.142
  48.0 1.7 copy.143
  49.7 1.7 copy.144
  51.5 1.7 copy.145
  53.2 1.7 copy.146
  55.0 1.7 copy.147
  56.7 1.7 copy.148
  58.4 1.8 copy.149
  60.2 1.7 copy.150
  61.9 1.7 copy.151
  63.7 1.7 copy.152
  65.4 1.7 copy.153
  67.2 1.7 copy.154
  68.9 1.8 copy.155
  70.7 1.7 copy.156
  72.4 1.1 copy.157
  73.5 1.1 copy.158
  74.7 1.1 copy.159
  75.8 1.1 copy.160
  77.0 1.1 copy.161
  78.1 1.1 copy.162
  79.2 1.1 copy.163
  101.0 6.8 %all-to-all-start = ((f32[32,1,160,4,8]{2,4,3,1,0:T(8,128)}), f32[32,1,160,4,8]{2,4,3,1,0:T(8,128)S(1)}, u32[]{:S(2)}, u32[]{:S(2)}) async-start(f32[32,1,160,4,8]{2,4,3,1,0:T(8,128)} %constant_dynamic-update-slice_fusion.3), calls=%async_computation | async-start | bytes 2097152 | tf_op jit(solution)/shard_map/all_to_all | solution.py:16
  114.0 21.0 %all-to-all-done = f32[32,1,160,4,8]{2,4,3,1,0:T(8,128)S(1)} async-done(((f32[32,1,160,4,8]{2,4,3,1,0:T(8,128)}), f32[32,1,160,4,8]{2,4,3,1,0:T(8,128)S(1)}, u32[]{:S(2)}, u32[]{:S(2)}) %all-to-all-start) | async-done | bytes 655392 | tf_op jit(solution)/shard_map/all_to_all | solution.py:16
  138.4 4.6 %collective-permute-start.5 = (f32[4,128]{1,0:T(4,128)S(1)}, f32[4,128]{1,0:T(4,128)S(1)}, u32[]{:S(2)}, u32[]{:S(2)}) collective-permute-start(f32[4,128]{1,0:T(4,128)S(1)} %pad_maximum_fusion.22), channel_id=1, source_target_pairs={{1,0},{2,1},{3,2},{4,3},{5,4},{6,5},{7,6},{8,7},{9,8},{10,9},{11,1... | collective-permute-start | bytes 6152 | tf_op jit(solution)/shard_map/ppermute | solution.py:31
  143.0 5.3 %collective-permute-start.3 = (f32[640,128]{1,0:T(8,128)S(1)}, f32[640,128]{1,0:T(8,128)S(1)}, u32[]{:S(2)}, u32[]{:S(2)}) collective-permute-start(f32[640,128]{1,0:T(8,128)S(1)} %subtract_bitcast_fusion), channel_id=1, source_target_pairs={{1,0},{2,1},{3,2},{4,3},{5,4},{6,5},{7,6},{8,7},{9,8},{10,9},{11,1... | collective-permute-start | bytes 983048 | tf_op jit(solution)/shard_map/ppermute | solution.py:31
  148.6 1.1 fusion.122
  150.4 5.9 %collective-permute-done.2 = f32[640,128]{1,0:T(8,128)S(1)} collective-permute-done((f32[640,128]{1,0:T(8,128)S(1)}, f32[640,128]{1,0:T(8,128)S(1)}, u32[]{:S(2)}, u32[]{:S(2)}) %collective-permute-start.2) | collective-permute-done | bytes 327712 | tf_op jit(solution)/shard_map/ppermute | solution.py:30
  156.3 2.3 %collective-permute-done.3 = f32[640,128]{1,0:T(8,128)S(1)} collective-permute-done((f32[640,128]{1,0:T(8,128)S(1)}, f32[640,128]{1,0:T(8,128)S(1)}, u32[]{:S(2)}, u32[]{:S(2)}) %collective-permute-start.3) | collective-permute-done | bytes 327712 | tf_op jit(solution)/shard_map/ppermute | solution.py:31
  166.3 1.6 fusion.10
  168.9 0.8 copy-done
  169.8 2.1 fusion.34
  172.6 1.1 fusion.42
  174.3 1.3 fusion.46
  177.1 1.2 fusion.32
  179.4 1.3 fusion.38
  182.2 0.9 fusion.28
  184.4 2.4 %fusion.104 = (f32[256]{0:T(256)S(1)}, pred[256]{0:T(512)(128)(4,1)S(1)}, pred[256]{0:T(512)(128)(4,1)S(1)}) fusion(f32[256]{0:T(256)S(1)} %add_reduce_fusion, f32[256]{0:T(256)S(1)} %copy-done.33, f32[256]{0:T(256)S(1)} %add_reduce_fusion.1, f32[]{:T(128)} %reduce_max.19, f32[]{:T(128)} %reduce_max.18, s32[]{:T(128)S(6)} %add.404, s32[]{:T(128)} %bitcast.38, ...), kind=kLoop, calls=%fused_computation.268 | loop fusion | flops 5120 | bytes 4632 | tf_op jit(solution)/shard_map/add | solution.py:134
  188.9 29.2 %all_to_all.20 = f32[32,160,4,8]{1,3,2,0:T(8,128)S(1)} all-to-all(f32[32,160,4,8]{1,3,2,0:T(8,128)S(1)} %bitcast.169), channel_id=1, replica_groups=mesh['member'=4,'lat'=8] {'member','lat'}, dimensions={0} | all-to-all | bytes 1310720 | tf_op jit(solution)/shard_map/all_to_all | solution.py:191
  218.2 1.1 copy.192
  (209 shorter events, 45.8 us)
Async XLA Ops:
  0.0 34.2 %copy-start.5 = (f32[160,4,256]{2,1,0:T(4,128)S(1)}, f32[160,4,256]{2,1,0:T(4,128)}, u32[]{:S(2)}) copy-start(f32[160,4,256]{2,1,0:T(4,128)} %param.6) | copy-start | bytes 1966084
  1.3 32.9 %collective-permute-start = (f32[160,4,256]{2,0,1:T(8,128)S(1)}, f32[160,4,256]{2,0,1:T(8,128)S(1)}, u32[]{:S(2)}, u32[]{:S(2)}) collective-permute-start(f32[160,4,256]{2,0,1:T(8,128)S(1)} %copy.139), channel_id=1, source_target_pairs={{0,1},{1,2},{2,3},{3,4},{4,5},{5,6},{6,7},{8,9},{9,10},{10,11},{11... | collective-permute-start | bytes 1966088 | tf_op jit(solution)/shard_map/ppermute | solution.py:30
  6.2 28.2 %collective-permute-start.1 = (f32[160,4,256]{2,0,1:T(8,128)S(1)}, f32[160,4,256]{2,0,1:T(8,128)S(1)}, u32[]{:S(2)}, u32[]{:S(2)}) collective-permute-start(f32[160,4,256]{2,0,1:T(8,128)S(1)} %copy.139), channel_id=1, source_target_pairs={{1,0},{2,1},{3,2},{4,3},{5,4},{6,5},{7,6},{9,8},{10,9},{11,10},{12... | collective-permute-start | bytes 1966088 | tf_op jit(solution)/shard_map/ppermute | solution.py:31
  80.6 1.6 copy-start.26
  80.6 2.2 %copy-start.27 = (f32[1,1,160,4,8]{2,4,3,1,0:T(8,128)S(1)}, f32[1,1,160,4,8]{2,4,3,1,0:T(8,128)}, u32[]{:S(2)}) copy-start(f32[1,1,160,4,8]{2,4,3,1,0:T(8,128)} %copy.144) | copy-start | bytes 61444
  80.6 2.8 %copy-start.25 = (f32[1,1,160,4,8]{2,4,3,1,0:T(8,128)S(1)}, f32[1,1,160,4,8]{2,4,3,1,0:T(8,128)}, u32[]{:S(2)}) copy-start(f32[1,1,160,4,8]{2,4,3,1,0:T(8,128)} %copy.145) | copy-start | bytes 61444
  80.6 3.4 %copy-start.24 = (f32[1,1,160,4,8]{2,4,3,1,0:T(8,128)S(1)}, f32[1,1,160,4,8]{2,4,3,1,0:T(8,128)}, u32[]{:S(2)}) copy-start(f32[1,1,160,4,8]{2,4,3,1,0:T(8,128)} %copy.146) | copy-start | bytes 61444
  80.7 3.9 %copy-start.23 = (f32[1,1,160,4,8]{2,4,3,1,0:T(8,128)S(1)}, f32[1,1,160,4,8]{2,4,3,1,0:T(8,128)}, u32[]{:S(2)}) copy-start(f32[1,1,160,4,8]{2,4,3,1,0:T(8,128)} %copy.147) | copy-start | bytes 61444
  80.7 4.5 %copy-start.22 = (f32[1,1,160,4,8]{2,4,3,1,0:T(8,128)S(1)}, f32[1,1,160,4,8]{2,4,3,1,0:T(8,128)}, u32[]{:S(2)}) copy-start(f32[1,1,160,4,8]{2,4,3,1,0:T(8,128)} %copy.148) | copy-start | bytes 61444
  80.7 5.1 %copy-start.21 = (f32[1,1,160,4,8]{2,4,3,1,0:T(8,128)S(1)}, f32[1,1,160,4,8]{2,4,3,1,0:T(8,128)}, u32[]{:S(2)}) copy-start(f32[1,1,160,4,8]{2,4,3,1,0:T(8,128)} %copy.149) | copy-start | bytes 61444
  80.7 5.7 %copy-start.20 = (f32[1,1,160,4,8]{2,4,3,1,0:T(8,128)S(1)}, f32[1,1,160,4,8]{2,4,3,1,0:T(8,128)}, u32[]{:S(2)}) copy-start(f32[1,1,160,4,8]{2,4,3,1,0:T(8,128)} %copy.150) | copy-start | bytes 61444
  80.8 6.3 %copy-start.19 = (f32[1,1,160,4,8]{2,4,3,1,0:T(8,128)S(1)}, f32[1,1,160,4,8]{2,4,3,1,0:T(8,128)}, u32[]{:S(2)}) copy-start(f32[1,1,160,4,8]{2,4,3,1,0:T(8,128)} %copy.151) | copy-start | bytes 61444
  80.9 6.7 %copy-start.18 = (f32[1,1,160,4,8]{2,4,3,1,0:T(8,128)S(1)}, f32[1,1,160,4,8]{2,4,3,1,0:T(8,128)}, u32[]{:S(2)}) copy-start(f32[1,1,160,4,8]{2,4,3,1,0:T(8,128)} %copy.152) | copy-start | bytes 61444
  80.9 7.3 %copy-start.16 = (f32[1,1,160,4,8]{2,4,3,1,0:T(8,128)S(1)}, f32[1,1,160,4,8]{2,4,3,1,0:T(8,128)}, u32[]{:S(2)}) copy-start(f32[1,1,160,4,8]{2,4,3,1,0:T(8,128)} %copy.153) | copy-start | bytes 61444
  80.9 7.9 %copy-start.17 = (f32[1,1,160,4,8]{2,4,3,1,0:T(8,128)S(1)}, f32[1,1,160,4,8]{2,4,3,1,0:T(8,128)}, u32[]{:S(2)}) copy-start(f32[1,1,160,4,8]{2,4,3,1,0:T(8,128)} %copy.154) | copy-start | bytes 61444
  80.9 8.5 %copy-start.15 = (f32[1,1,160,4,8]{2,4,3,1,0:T(8,128)S(1)}, f32[1,1,160,4,8]{2,4,3,1,0:T(8,128)}, u32[]{:S(2)}) copy-start(f32[1,1,160,4,8]{2,4,3,1,0:T(8,128)} %copy.155) | copy-start | bytes 61444
  81.0 9.1 %copy-start.14 = (f32[1,1,160,4,8]{2,4,3,1,0:T(8,128)S(1)}, f32[1,1,160,4,8]{2,4,3,1,0:T(8,128)}, u32[]{:S(2)}) copy-start(f32[1,1,160,4,8]{2,4,3,1,0:T(8,128)} %copy.156) | copy-start | bytes 61444
  90.1 17.7 %copy-start.38 = (s32[1,2]{1,0:T(1,128)S(1)}, s32[1,2]{1,0:T(1,128)}, u32[]{:S(2)}) copy-start(s32[1,2]{1,0:T(1,128)} %param.10) | copy-start | bytes 28
  90.7 23.2 %copy-start.40 = (s32[1,128]{1,0:T(1,128)S(1)}, s32[1,128]{1,0:T(1,128)}, u32[]{:S(2)}) copy-start(s32[1,128]{1,0:T(1,128)} %param.7) | copy-start | bytes 1540
  90.7 23.3 %copy-start.36 = (f32[3]{0:T(128)S(1)}, f32[3]{0:T(128)}, u32[]{:S(2)}) copy-start(f32[3]{0:T(128)} %constant.157) | copy-start | bytes 40
  101.0 34.1 %all-to-all-start = ((f32[32,1,160,4,8]{2,4,3,1,0:T(8,128)}), f32[32,1,160,4,8]{2,4,3,1,0:T(8,128)S(1)}, u32[]{:S(2)}, u32[]{:S(2)}) async-start(f32[32,1,160,4,8]{2,4,3,1,0:T(8,128)} %constant_dynamic-update-slice_fusion.3), calls=%async_computation | async-start | bytes 2097152 | tf_op jit(solution)/shard_map/all_to_all | solution.py:16
  136.4 1.1 copy-start.41
  136.4 1.1 copy-start.39
  137.5 12.4 %collective-permute-start.4 = (f32[4,128]{1,0:T(4,128)S(1)}, f32[4,128]{1,0:T(4,128)S(1)}, u32[]{:S(2)}, u32[]{:S(2)}) collective-permute-start(f32[4,128]{1,0:T(4,128)S(1)} %pad_maximum_fusion.22), channel_id=1, source_target_pairs={{0,1},{1,2},{2,3},{3,4},{4,5},{5,6},{6,7},{7,8},{8,9},{9,10},{10,1... | collective-permute-start | bytes 6152 | tf_op jit(solution)/shard_map/ppermute | solution.py:30
  138.4 11.6 %collective-permute-start.5 = (f32[4,128]{1,0:T(4,128)S(1)}, f32[4,128]{1,0:T(4,128)S(1)}, u32[]{:S(2)}, u32[]{:S(2)}) collective-permute-start(f32[4,128]{1,0:T(4,128)S(1)} %pad_maximum_fusion.22), channel_id=1, source_target_pairs={{1,0},{2,1},{3,2},{4,3},{5,4},{6,5},{7,6},{8,7},{9,8},{10,9},{11,1... | collective-permute-start | bytes 6152 | tf_op jit(solution)/shard_map/ppermute | solution.py:31
  143.0 23.3 %copy-start.8 = (f32[640,128]{1,0:T(8,128)}, f32[640,128]{1,0:T(8,128)S(1)}, u32[]{:S(2)}) copy-start(f32[640,128]{1,0:T(8,128)S(1)} %subtract_bitcast_fusion) | copy-start | bytes 983044
  143.0 13.4 %collective-permute-start.2 = (f32[640,128]{1,0:T(8,128)S(1)}, f32[640,128]{1,0:T(8,128)S(1)}, u32[]{:S(2)}, u32[]{:S(2)}) collective-permute-start(f32[640,128]{1,0:T(8,128)S(1)} %subtract_bitcast_fusion), channel_id=1, source_target_pairs={{0,1},{1,2},{2,3},{3,4},{4,5},{5,6},{6,7},{7,8},{8,9},{9,10},{10,1... | collective-permute-start | bytes 983048 | tf_op jit(solution)/shard_map/ppermute | solution.py:30
  143.0 15.6 %collective-permute-start.3 = (f32[640,128]{1,0:T(8,128)S(1)}, f32[640,128]{1,0:T(8,128)S(1)}, u32[]{:S(2)}, u32[]{:S(2)}) collective-permute-start(f32[640,128]{1,0:T(8,128)S(1)} %subtract_bitcast_fusion), channel_id=1, source_target_pairs={{1,0},{2,1},{3,2},{4,3},{5,4},{6,5},{7,6},{8,7},{9,8},{10,9},{11,1... | collective-permute-start | bytes 983048 | tf_op jit(solution)/shard_map/ppermute | solution.py:31
  149.8 9.5 %copy-start.32 = (f32[256]{0:T(256)}, f32[256]{0:T(256)S(1)}, u32[]{:S(2)}) copy-start(f32[256]{0:T(256)S(1)} %div.166) | copy-start | bytes 3076
  149.9 16.4 %copy-start.6 = (f32[640,256]{1,0:T(8,128)}, f32[640,256]{1,0:T(8,128)S(1)}, u32[]{:S(2)}) copy-start(f32[640,256]{1,0:T(8,128)S(1)} %broadcast_subtract_fusion) | copy-start | bytes 1966084
  150.0 14.9 %copy-start.28 = (f32[1,384]{1,0:T(1,128)}, f32[1,384]{1,0:T(1,128)S(1)}, u32[]{:S(2)}) copy-start(f32[1,384]{1,0:T(1,128)S(1)} %get-tuple-element.84) | copy-start | bytes 4612
  150.4 13.8 %copy-start.30 = (f32[1,384]{1,0:T(1,128)}, f32[1,384]{1,0:T(1,128)S(1)}, u32[]{:S(2)}) copy-start(f32[1,384]{1,0:T(1,128)S(1)} %get-tuple-element.26) | copy-start | bytes 4612
  156.3 9.9 %copy-start.10 = (f32[640,128]{1,0:T(8,128)}, f32[640,128]{1,0:T(8,128)S(1)}, u32[]{:S(2)}) copy-start(f32[640,128]{1,0:T(8,128)S(1)} %collective-permute-done.2) | copy-start | bytes 983044
  158.6 7.7 %copy-start.12 = (f32[640,128]{1,0:T(8,128)}, f32[640,128]{1,0:T(8,128)S(1)}, u32[]{:S(2)}) copy-start(f32[640,128]{1,0:T(8,128)S(1)} %collective-permute-done.3) | copy-start | bytes 983044
  160.7 4.8 %copy-start.37 = (f32[3]{0:T(128)S(1)}, f32[3]{0:T(128)}, u32[]{:S(2)}) copy-start(f32[3]{0:T(128)} %constant.157) | copy-start | bytes 40
  168.9 0.8 copy-start
  171.9 1.9 copy-start.1
  171.9 1.9 copy-start.2
  182.1 1.3 copy-start.29
  182.1 1.3 copy-start.31
  183.1 1.1 copy-start.4
  183.3 1.1 copy-start.33
  183.3 3.5 %copy-start.7 = (f32[640,256]{1,0:T(8,128)S(1)}, f32[640,256]{1,0:T(8,128)}, u32[]{:S(2)}) copy-start(f32[640,256]{1,0:T(8,128)} %copy-done.6) | copy-start | bytes 1966084
  183.3 3.5 %copy-start.9 = (f32[640,128]{1,0:T(8,128)S(1)}, f32[640,128]{1,0:T(8,128)}, u32[]{:S(2)}) copy-start(f32[640,128]{1,0:T(8,128)} %copy-done.8) | copy-start | bytes 983044
  183.3 3.5 %copy-start.11 = (f32[640,128]{1,0:T(8,128)S(1)}, f32[640,128]{1,0:T(8,128)}, u32[]{:S(2)}) copy-start(f32[640,128]{1,0:T(8,128)} %copy-done.10) | copy-start | bytes 983044
  183.3 3.5 %copy-start.13 = (f32[640,128]{1,0:T(8,128)S(1)}, f32[640,128]{1,0:T(8,128)}, u32[]{:S(2)}) copy-start(f32[640,128]{1,0:T(8,128)} %copy-done.12) | copy-start | bytes 983044
  183.3 3.5 %copy-start.34 = (f32[384]{0:T(512)S(1)}, f32[384]{0:T(512)}, u32[]{:S(2)}) copy-start(f32[384]{0:T(512)} %get-tuple-element.12) | copy-start | bytes 4612
  183.3 3.5 %copy-start.35 = (f32[384]{0:T(512)S(1)}, f32[384]{0:T(512)}, u32[]{:S(2)}) copy-start(f32[384]{0:T(512)} %get-tuple-element.86) | copy-start | bytes 4612
  (1 other events, 0.8 us)
